TPU v7x, 32 devices: a whole 2x2x4 slice. The times are simulated.
32 devices in a mesh: dp: 4 (over x, core), vocab: 8 (over z, y).
Axes of the slice: x: 2, y: 2, z: 4, core: 2. Of those that a mesh axis runs over, the one named last changes fastest.
Arguments:
- hidden: bfloat16 [1024, 2048], P('dp', 'vocab'), may hold values from -30 to 30
- table: bfloat16 [16000, 2048], P('vocab'), may hold values from -20 to 20
- targets: int32 [1024], P('dp'), may hold values from 0 to 15999
- input_ids: int32 [2048], P(('dp', 'vocab')), may hold values from 0 to 15999, as said below
- cotangent: bfloat16 [2048, 2048], P(('dp', 'vocab')), may hold values from -0.4375 to 0.4375
Outputs:
- token_loss: float32 [1024], P('dp')
- hidden_grad: bfloat16 [1024, 2048], P('dp', 'vocab')
- table_grad: bfloat16 [16000, 2048], P('vocab', 'dp')
Inputs may be any that keep to these rules, and one draw needn't show every extreme that they name: `input_ids`: within the 64 rows of one device, at most 16 ids fall in any one block of 2000 consecutive ids (the rows of one index of vocab); in every draw some block receives exactly 16 ids from every device.
All inputs are finite; a program needn't handle non-finite values.
Results may differ from a plain program's by a relative error of at most 0.0034.
Values may be sent and summed in bfloat16 or wider, within the bound.
A program may use at most 128 MiB of HBM per device.

v0:
```python
import jax
import jax.numpy as jnp
from jax import lax
from jax.sharding import PartitionSpec as P


def body(hidden, table, targets, input_ids, cotangent):
    vocab_rows = table.shape[0]
    model_width = table.shape[1]
    data_count = lax.axis_size("dp")
    vocab_count = lax.axis_size("vocab")
    first_row = lax.axis_index("vocab") * vocab_rows
    hidden_full = lax.all_gather(hidden, "vocab", axis=1, tiled=True)
    logits = lax.dot_general(
        hidden_full, table, (((1,), (1,)), ((), ())), preferred_element_type=jnp.float32
    )
    columns = lax.broadcasted_iota(jnp.int32, logits.shape, 1)
    is_target = columns == (targets - first_row)[:, None]
    picked = jnp.sum(jnp.where(is_target, logits, 0.0), axis=1)
    local_max = jnp.max(logits, axis=1)
    row_max = lax.pmax(local_max, "vocab")
    shifted = jnp.exp(logits - row_max[:, None])
    row_sum, target_logit = lax.psum((jnp.sum(shifted, axis=1), picked), "vocab")
    token_loss = row_max + jnp.log(row_sum) - target_logit
    residual = (shifted / row_sum[:, None] - jnp.where(is_target, 1.0, 0.0)).astype(jnp.bfloat16)
    hidden_part = jnp.dot(residual, table, preferred_element_type=jnp.float32)
    hidden_grad = lax.psum_scatter(hidden_part, "vocab", scatter_dimension=1, tiled=True).astype(
        jnp.bfloat16
    )
    row_count = input_ids.shape[0]
    capacity = max(2, 2 * row_count // vocab_count)
    slot_total = vocab_count * capacity
    owners = input_ids // vocab_rows
    offsets = input_ids - owners * vocab_rows
    later_rows = lax.broadcasted_iota(jnp.int32, (row_count, row_count), 0)
    earlier_rows = lax.broadcasted_iota(jnp.int32, (row_count, row_count), 1)
    earlier = (owners[:, None] == owners[None, :]) & (earlier_rows < later_rows)
    position = jnp.sum(earlier.astype(jnp.int32), axis=1)
    slot_index = owners * capacity + position
    selector = lax.broadcasted_iota(jnp.int32, (slot_total, row_count), 0) == slot_index[None, :]
    send_rows = jnp.dot(
        selector.astype(jnp.bfloat16), cotangent, preferred_element_type=jnp.float32
    ).astype(jnp.bfloat16)
    send_rows = send_rows.reshape(vocab_count, capacity, model_width)
    send_offsets = jnp.sum(jnp.where(selector, offsets[None, :] + 1, 0), axis=1) - 1
    offset_copies = jnp.broadcast_to(
        send_offsets.reshape(vocab_count, capacity, 1), (vocab_count, capacity, data_count)
    )
    got_rows, got_offsets = (
        lax.all_to_all(
            lax.all_to_all(send_rows, "dp", split_axis=2, concat_axis=1, tiled=True),
            "vocab",
            split_axis=0,
            concat_axis=0,
            tiled=True,
        ),
        lax.all_to_all(
            lax.all_to_all(offset_copies, "dp", split_axis=2, concat_axis=1, tiled=True),
            "vocab",
            split_axis=0,
            concat_axis=0,
            tiled=True,
        ),
    )
    block_width = model_width // data_count
    flat_rows = got_rows.reshape(-1, block_width)
    flat_offsets = got_offsets.reshape(-1)
    matches = (
        lax.broadcasted_iota(jnp.int32, (vocab_rows, flat_offsets.shape[0]), 0)
        == flat_offsets[None, :]
    )
    start_sum = jnp.dot(matches.astype(jnp.bfloat16), flat_rows, preferred_element_type=jnp.float32)
    hidden_block = lax.all_to_all(hidden_full, "dp", split_axis=1, concat_axis=0, tiled=True)
    table_sum = start_sum + lax.dot_general(
        lax.all_gather(residual, "dp", axis=0, tiled=True),
        hidden_block,
        (((0,), (0,)), ((), ())),
        preferred_element_type=jnp.float32,
    )
    return (token_loss, hidden_grad, table_sum.astype(jnp.bfloat16))


def solution(mesh):
    placed = (
        P("dp", "vocab"),
        P("vocab", None),
        P("dp"),
        P(("dp", "vocab")),
        P(("dp", "vocab"), None),
    )
    return jax.shard_map(
        body,
        mesh=mesh,
        in_specs=placed,
        out_specs=(P("dp"), P("dp", "vocab"), P("vocab", "dp")),
        check_vma=False,
    )
```

profile of v0, /device:TPU:0, one launch (start us, length us, event | category | flops | bytes accessed | tf_op | source)
XLA Modules:
  0.0 228.6 jit_solution(13817739331604094054)
XLA Ops:
  7.2 0.0 copy-start
  7.2 0.0 all-gather.3.cloned.1.call-start
  7.2 1.7 copy.18
  8.9 0.0 all-gather.3.cloned.1.call-update
  8.9 0.0 reduce-scatter.2.cloned.1.call-start
  9.0 0.7 broadcast_subtract_fusion
  9.7 44.0 %all-gather.3.cloned.1.call-done = bf16[256,2048]{0,1:T(8,128)(2,1)} async-done(((bf16[256,256]{0,1:T(8,128)(2,1)}), bf16[256,2048]{0,1:T(8,128)(2,1)}) %all-gather.3.cloned.1.call-update) | async-done | bytes 1048592 | tf_op jit(solution)/shard_map/all_gather | solution.py:13
  53.7 5.9 %fusion.5 = (f32[256]{0:T(256)S(1)}, f32[256,2000]{0,1:T(8,128)S(1)}) fusion(bf16[2000,2048]{1,0:T(8,128)(2,1)} %param.6, bf16[256,2048]{0,1:T(8,128)(2,1)} %all-gather.3.cloned.1.call-done), kind=kOutput, calls=%fused_computation.22 | convolution fusion | flops 2097663744 | bytes 11289600 | tf_op jit(solution)/shard_map/dot_general | solution.py:14
  59.6 19.2 %pmax.7 = f32[256]{0:T(256)S(1)} all-reduce(f32[256]{0:T(256)S(1)} %get-tuple-element.9), channel_id=1, replica_groups=mesh['dp'=4,'vocab'=8] {'vocab'}, use_global_device_ids=true, to_apply=%region_1.2 | all-reduce | flops 256 | bytes 2048 | tf_op jit(solution)/shard_map/pmax | solution.py:21
  78.7 0.6 fusion.2
  79.3 17.1 %all-reduce = (f32[256]{0:T(256)S(1)}, f32[256]{0:T(256)S(1)}) all-reduce(f32[256]{0:T(256)S(1)} %get-tuple-element.4, f32[256]{0:T(256)S(1)} %get-tuple-element.3), channel_id=1, replica_groups=mesh['dp'=4,'vocab'=8] {'vocab'}, use_global_device_ids=true, to_apply=%region_5.6 | all-reduce | flops 512 | bytes 4096 | tf_op jit(solution)/shard_map/psum | solution.py:23
  96.4 0.6 subtract_convert_fusion
  97.0 0.0 copy-start.1
  97.0 7.4 %fusion.6 = f32[256,2048]{1,0:T(8,128)} fusion(bf16[256,2000]{0,1:T(8,128)(2,1)S(1)} %subtract_convert_fusion, bf16[2000,2048]{1,0:T(8,128)(2,1)} %param.6), kind=kOutput, calls=%fused_computation.25 | convolution fusion | flops 2097152000 | bytes 11313152 | tf_op jit(solution)/shard_map/dot_general | solution.py:26
  104.4 0.0 copy-done.1
  104.4 0.0 copy-start.2
  104.4 0.0 reduce-scatter.2.cloned.1.call-update
  104.5 0.0 all-gather.5.cloned.1.call-start
  104.5 0.7 all-gather.5.cloned.1.call-update
  105.2 0.0 copy-done.2
  105.2 0.2 convert_reduce_fusion
  105.4 0.1 select_reduce_fusion.1
  105.5 0.1 sub.44
  105.6 0.7 reshape.45
  106.3 3.2 %all-to-all-start = ((s32[4,1,128]{2,1,0:T(1,128)}), s32[4,1,128]{2,1,0:T(1,128)S(1)}, u32[]{:S(2)}, u32[]{:S(2)}) async-start(s32[4,1,128]{2,1,0:T(1,128)} %reshape.45), calls=%async_computation.1 | async-start | bytes 4096 | tf_op jit(solution)/shard_map/all_to_all | solution.py:58
  109.5 0.0 copy-done
  109.5 0.4 convolution_convert_fusion
  109.9 4.2 %copy.21 = bf16[8,16,2048]{1,0,2:T(8,128)(2,1)} copy(bf16[8,16,2048]{2,1,0:T(8,128)(2,1)S(1)} %bitcast.33) | data formatting | bytes 1048576 | tf_op jit(solution)/shard_map/reshape | solution.py:44
  114.1 6.5 %reshape.43 = bf16[4,2,32768]{2,1,0:T(2,128)(2,1)} reshape(bf16[2048,8,16]{2,1,0:T(8,128)(2,1)} %bitcast.30) | data formatting | bytes 1048576
  120.6 0.0 all-to-all-done
  120.6 3.5 %all-to-all-start.2 = ((bf16[4,2,32768]{2,1,0:T(2,128)(2,1)}), bf16[4,2,32768]{2,1,0:T(2,128)(2,1)S(1)}, u32[]{:S(2)}, u32[]{:S(2)}) async-start(bf16[4,2,32768]{2,1,0:T(2,128)(2,1)} %reshape.43), calls=%async_computation.3 | async-start | bytes 1048576 | tf_op jit(solution)/shard_map/all_to_all | solution.py:51
  124.1 0.5 broadcast.29
  124.6 0.7 reduce.4
  125.3 0.1 reshape.46
  125.4 0.7 all_to_all.49
  126.0 6.8 %all-to-all-done.2 = bf16[4,2,32768]{2,1,0:T(2,128)(2,1)S(1)} async-done(((bf16[4,2,32768]{2,1,0:T(2,128)(2,1)}), bf16[4,2,32768]{2,1,0:T(2,128)(2,1)S(1)}, u32[]{:S(2)}, u32[]{:S(2)}) %all-to-all-start.2) | async-done | bytes 524320 | tf_op jit(solution)/shard_map/all_to_all | solution.py:51
  132.9 3.3 %all-to-all-start.1 = ((s32[8,64,1]{1,2,0:T(1,128)}), s32[8,64,1]{1,2,0:T(1,128)S(1)}, u32[]{:S(2)}, u32[]{:S(2)}) async-start(s32[8,64,1]{1,2,0:T(1,128)} %bitcast.2), calls=%async_computation.2 | async-start | bytes 8192 | tf_op jit(solution)/shard_map/all_to_all | solution.py:57
  136.2 4.1 %reshape.44 = bf16[2048,8,16]{2,1,0:T(8,128)(2,1)} reshape(bf16[4,2,32768]{2,1,0:T(2,128)(2,1)S(1)} %all-to-all-done.2) | data formatting | bytes 1048576
  140.3 4.9 %copy.25 = bf16[8,16,4,512]{3,2,1,0:T(4,128)(2,1)S(1)} copy(bf16[8,16,4,512]{1,0,3,2:T(8,128)(2,1)} %bitcast.31) | data formatting | bytes 1048576 | tf_op jit(solution)/shard_map/all_to_all | solution.py:51
  145.2 0.1 copy.23
  145.3 0.0 all-to-all-done.1
  145.3 27.8 %all_to_all.65 = bf16[8,64,512]{2,1,0:T(8,128)(2,1)S(1)} all-to-all(bf16[8,64,512]{2,1,0:T(8,128)(2,1)S(1)} %bitcast.35), channel_id=1, replica_groups=mesh['dp'=4,'vocab'=8] {'vocab'}, dimensions={0} | all-to-all | bytes 1048576 | tf_op jit(solution)/shard_map/all_to_all | solution.py:50
  173.1 3.7 %all-to-all-start.4 = ((bf16[256,4,512]{0,2,1:T(8,128)(2,1)}), bf16[256,4,512]{0,2,1:T(8,128)(2,1)S(1)}, u32[]{:S(2)}, u32[]{:S(2)}) async-start(bf16[256,4,512]{0,2,1:T(8,128)(2,1)} %bitcast.8), calls=%async_computation.5 | async-start | bytes 2097152 | tf_op jit(solution)/shard_map/all_to_all | solution.py:73
  176.8 0.5 broadcast.27
  177.3 0.7 reduce.3
  178.0 0.1 eq.46
  178.1 3.1 %fusion = f32[2000,512]{1,0:T(8,128)} fusion(bf16[512,512]{1,0:T(8,128)(2,1)S(1)} %bitcast.37, s32[512]{0:T(512)S(1)} %eq.46), kind=kOutput, calls=%fused_computation.2 | convolution fusion | flops 1049600000 | bytes 4622336 | tf_op jit(solution)/shard_map/dot_general | solution.py:72
  181.2 0.6 add_subtract_fusion
  181.8 14.4 %all-to-all-done.4 = bf16[256,4,512]{0,2,1:T(8,128)(2,1)S(1)} async-done(((bf16[256,4,512]{0,2,1:T(8,128)(2,1)}), bf16[256,4,512]{0,2,1:T(8,128)(2,1)S(1)}, u32[]{:S(2)}, u32[]{:S(2)}) %all-to-all-start.4) | async-done | bytes 1048608 | tf_op jit(solution)/shard_map/all_to_all | solution.py:73
  196.1 0.5 copy.24
  196.7 0.0 reduce-scatter.2.cloned.1.call-done
  196.7 1.6 convert_element_type.18
  198.3 16.8 %all-gather.5.cloned.1.call-done = bf16[1024,2000]{0,1:T(8,128)(2,1)} async-done(((bf16[256,2000]{0,1:T(8,128)(2,1)}), bf16[1024,2000]{0,1:T(8,128)(2,1)}) %all-gather.5.cloned.1.call-update) | async-done | bytes 4096016 | tf_op jit(solution)/shard_map/all_gather | solution.py:75
  215.1 7.0 %add_convert_fusion = bf16[2000,512]{1,0:T(8,128)(2,1)} fusion(f32[2000,512]{1,0:T(8,128)} %fusion, bf16[1024,2000]{0,1:T(8,128)(2,1)} %all-gather.5.cloned.1.call-done, bf16[1024,512]{1,0:T(8,128)(2,1)S(1)} %bitcast.36), kind=kOutput, calls=%fused_computation | convolution fusion | flops 2099200000 | bytes 11288576 | tf_op jit(solution)/shard_map/dot_general | solution.py:74
  (6 shorter events, 0.0 us)
Async XLA Ops:
  7.2 102.4 %copy-start = (bf16[64,2048]{1,0:T(8,128)(2,1)S(1)}, bf16[64,2048]{1,0:T(8,128)(2,1)}, u32[]{:S(2)}) copy-start(bf16[64,2048]{1,0:T(8,128)(2,1)} %param.9) | copy-start | bytes 786436
  7.2 46.5 %all-gather.3.cloned.1.call-start = ((), (), s32[]{:S(2)}) async-start(), calls=%async_computation.6 | async-start | bytes 1179648 | tf_op jit(solution)/shard_map/all_gather | solution.py:13
  8.9 187.8 %reduce-scatter.2.cloned.1.call-start = ((), (), s32[]{:S(2)}) async-start(), calls=%async_computation.7 | async-start | bytes 2359296 | tf_op jit(solution)/shard_map/reduce_scatter | solution.py:27
  97.0 7.4 %copy-start.1 = (bf16[256,2000]{0,1:T(8,128)(2,1)}, bf16[256,2000]{0,1:T(8,128)(2,1)S(1)}, u32[]{:S(2)}) copy-start(bf16[256,2000]{0,1:T(8,128)(2,1)S(1)} %subtract_convert_fusion) | copy-start | bytes 3072004
  104.4 0.8 copy-start.2
  104.5 110.7 %all-gather.5.cloned.1.call-start = ((), (), s32[]{:S(2)}) async-start(), calls=%async_computation.8 | async-start | bytes 5120000 | tf_op jit(solution)/shard_map/all_gather | solution.py:75
  106.3 14.3 %all-to-all-start = ((s32[4,1,128]{2,1,0:T(1,128)}), s32[4,1,128]{2,1,0:T(1,128)S(1)}, u32[]{:S(2)}, u32[]{:S(2)}) async-start(s32[4,1,128]{2,1,0:T(1,128)} %reshape.45), calls=%async_computation.1 | async-start | bytes 4096 | tf_op jit(solution)/shard_map/all_to_all | solution.py:58
  120.6 12.3 %all-to-all-start.2 = ((bf16[4,2,32768]{2,1,0:T(2,128)(2,1)}), bf16[4,2,32768]{2,1,0:T(2,128)(2,1)S(1)}, u32[]{:S(2)}, u32[]{:S(2)}) async-start(bf16[4,2,32768]{2,1,0:T(2,128)(2,1)} %reshape.43), calls=%async_computation.3 | async-start | bytes 1048576 | tf_op jit(solution)/shard_map/all_to_all | solution.py:51
  132.9 12.5 %all-to-all-start.1 = ((s32[8,64,1]{1,2,0:T(1,128)}), s32[8,64,1]{1,2,0:T(1,128)S(1)}, u32[]{:S(2)}, u32[]{:S(2)}) async-start(s32[8,64,1]{1,2,0:T(1,128)} %bitcast.2), calls=%async_computation.2 | async-start | bytes 8192 | tf_op jit(solution)/shard_map/all_to_all | solution.py:57
  173.1 23.0 %all-to-all-start.4 = ((bf16[256,4,512]{0,2,1:T(8,128)(2,1)}), bf16[256,4,512]{0,2,1:T(8,128)(2,1)S(1)}, u32[]{:S(2)}, u32[]{:S(2)}) async-start(bf16[256,4,512]{0,2,1:T(8,128)(2,1)} %bitcast.8), calls=%async_computation.5 | async-start | bytes 2097152 | tf_op jit(solution)/shard_map/all_to_all | solution.py:73
Sparse Core Ops, SparseCore 0:
  10.7 42.9 all-gather.2
  104.6 70.6 reduce-scatter.1
  177.4 37.6 all-gather.4
where the time goes:
time: 229 us
  waiting for transfers between devices  82.8 us (36%)
  blocking collectives  64 us (28%)
  local copies, waits for them, and re-layouts  24.7 us (11%)
  matrix products  23.8 us (10%)
  between operations  13.9 us (6%)
  starting transfers between devices  13.8 us (6%)
  other arithmetic  5.64 us (2%)
    all_gather x1, waiting for transfers between devices, body(): hidden_full = lax.all_gather(hidden, 'vocab', axis=1, tiled=True)  44 us
    all_to_all x1, blocking collectives, body(): lax.all_to_all(lax.all_to_all(send_rows, 'dp', split_axis=2, concat_axis=...  27.8 us
    pmax x1, blocking collectives, body(): row_max = lax.pmax(local_max, 'vocab')  19.2 us
    psum x1, blocking collectives, body(): lax.psum((jnp.sum(shifted, axis=1), picked), 'vocab')  17.1 us
    all_gather x1, waiting for transfers between devices, body(): lax.all_gather(residual, 'dp', axis=0, tiled=True)  16.8 us
    all_to_all x1, waiting for transfers between devices, body(): lax.all_to_all(hidden_full, 'dp', split_axis=1, concat_axis=0, tiled=True)  14.4 us
    unnamed x12, local copies, waits for them, and re-layouts  13.1 us
    dot_general x1, matrix products, body(): hidden_part = jnp.dot(residual, table, preferred_element_type=jnp.float32)  7.42 us
  transfers between devices with their start and end apart: 7, of which 4 were waited for; matrix products, arithmetic and copies ran while one was open for 13% of the time, Pallas kernels for 0%

commit v1 on v0

--- a/solution.py
+++ b/solution.py
@@ -48,7 +48,12 @@
     )
     got_rows, got_offsets = (
         lax.all_to_all(
-            lax.all_to_all(send_rows, "dp", split_axis=2, concat_axis=1, tiled=True),
+            jnp.concatenate(
+                lax.all_to_all(
+                    jnp.stack(jnp.split(send_rows, lax.axis_size("dp"), axis=2)), "dp", 0, 0
+                ),
+                axis=1,
+            ),
             "vocab",
             split_axis=0,
             concat_axis=0,

time: 229 us -> 223 us (0.974)
  waiting for transfers between devices: 82.8 us -> 108 us
  local copies, waits for them, and re-layouts: 24.7 us -> 4.97 us
  blocking collectives: 64 us -> 52 us
    all_gather x1, waiting for transfers between devices: 16.8 us -> 34 us  [body(): lax.all_gather(residual, 'dp', axis=0, tiled=True)]
    all_to_all x1, blocking collectives: 27.8 us -> 15.7 us  [body(): lax.all_to_all(jnp.concatenate(lax.all_to_all(jnp.stack(jnp.split(send_ro...]
    unnamed x12 -> x10, local copies, waits for them, and re-layouts: 13.1 us -> 2.47 us
    all_to_all x1, waiting for transfers between devices: 0.01 us -> 6.35 us  [body(): lax.all_to_all(lax.all_to_all(offset_copies, 'dp', split_axis=2, concat_a...]
    all_to_all x2 -> x1, local copies, waits for them, and re-layouts: 4.98 us -> 0.04 us  [body(): lax.all_to_all(jnp.stack(jnp.split(send_rows, lax.axis_size('dp'), axis=2...]
    all_to_all x1, waiting for transfers between devices: 14.4 us -> 9.44 us  [body(): lax.all_to_all(hidden_full, 'dp', split_axis=1, concat_axis=0, tiled=True)]
    reduce_scatter x1, waiting for transfers between devices: 0.02 us -> 4.41 us  [body(): lax.psum_scatter(hidden_part, 'vocab', scatter_dimension=1, tiled=True)]
    reshape x1 -> x0, local copies, waits for them, and re-layouts: 4.19 us -> none  [body(): send_rows = send_rows.reshape(vocab_count, capacity, model_width)]
  transfers between devices with their start and end apart: 7 -> 7, of which waited for: 4 -> 7; matrix products, arithmetic and copies ran while one was open for 13% -> 5% of each run, Pallas kernels for 0% -> 0%
where the time goes in v1:
time: 223 us
  waiting for transfers between devices  108 us (48%)
  blocking collectives  52 us (23%)
  matrix products  23.9 us (11%)
  between operations  13.9 us (6%)
  starting transfers between devices  13.6 us (6%)
  other arithmetic  6.49 us (3%)
  local copies, waits for them, and re-layouts  4.97 us (2%)
    all_gather x1, waiting for transfers between devices, body(): hidden_full = lax.all_gather(hidden, 'vocab', axis=1, tiled=True)  44 us
    all_gather x1, waiting for transfers between devices, body(): lax.all_gather(residual, 'dp', axis=0, tiled=True)  34 us
    pmax x1, blocking collectives, body(): row_max = lax.pmax(local_max, 'vocab')  19.2 us
    psum x1, blocking collectives, body(): lax.psum((jnp.sum(shifted, axis=1), picked), 'vocab')  17.1 us
    all_to_all x1, blocking collectives, body(): lax.all_to_all(jnp.concatenate(lax.all_to_all(jnp.stack(jnp.split(send_ro...  15.7 us
    all_to_all x1, waiting for transfers between devices, body(): lax.all_to_all(hidden_full, 'dp', split_axis=1, concat_axis=0, tiled=True)  9.44 us
    dot_general x1, matrix products, body(): hidden_part = jnp.dot(residual, table, preferred_element_type=jnp.float32)  7.45 us
    dot_general x1, matrix products, body(): lax.dot_general(lax.all_gather(residual, 'dp', axis=0, tiled=True), hidde...  7 us
  transfers between devices with their start and end apart: 7, of which 7 were waited for; matrix products, arithmetic and copies ran while one was open for 5% of the time, Pallas kernels for 0%

profile of v1, /device:TPU:0, one launch (start us, length us, event | category | flops | bytes accessed | tf_op | source)
XLA Modules:
  0.0 222.9 jit_solution(5920416043830929619)
XLA Ops:
  7.2 0.0 copy-start
  7.2 0.0 all-gather.3.cloned.1.call-start
  7.2 1.7 copy.21
  8.9 0.0 all-gather.3.cloned.1.call-update
  8.9 0.0 reduce-scatter.2.cloned.1.call-start
  9.0 0.7 broadcast_subtract_fusion
  9.7 44.0 %all-gather.3.cloned.1.call-done = bf16[256,2048]{0,1:T(8,128)(2,1)} async-done(((bf16[256,256]{0,1:T(8,128)(2,1)}), bf16[256,2048]{0,1:T(8,128)(2,1)}) %all-gather.3.cloned.1.call-update) | async-done | bytes 1048592 | tf_op jit(solution)/shard_map/all_gather | solution.py:13
  53.7 5.9 %fusion.5 = (f32[256]{0:T(256)S(1)}, f32[256,2000]{0,1:T(8,128)S(1)}) fusion(bf16[2000,2048]{1,0:T(8,128)(2,1)} %param.6, bf16[256,2048]{0,1:T(8,128)(2,1)} %all-gather.3.cloned.1.call-done), kind=kOutput, calls=%fused_computation.27 | convolution fusion | flops 2097663744 | bytes 11289600 | tf_op jit(solution)/shard_map/dot_general | solution.py:14
  59.6 19.2 %pmax.7 = f32[256]{0:T(256)S(1)} all-reduce(f32[256]{0:T(256)S(1)} %get-tuple-element.13), channel_id=1, replica_groups=mesh['dp'=4,'vocab'=8] {'vocab'}, use_global_device_ids=true, to_apply=%region_1.2 | all-reduce | flops 256 | bytes 2048 | tf_op jit(solution)/shard_map/pmax | solution.py:21
  78.7 0.6 fusion.2
  79.3 17.1 %all-reduce = (f32[256]{0:T(256)S(1)}, f32[256]{0:T(256)S(1)}) all-reduce(f32[256]{0:T(256)S(1)} %get-tuple-element.4, f32[256]{0:T(256)S(1)} %get-tuple-element.3), channel_id=1, replica_groups=mesh['dp'=4,'vocab'=8] {'vocab'}, use_global_device_ids=true, to_apply=%region_5.6 | all-reduce | flops 512 | bytes 4096 | tf_op jit(solution)/shard_map/psum | solution.py:23
  96.4 0.6 subtract_convert_fusion
  97.0 0.0 copy-start.1
  97.0 7.5 %fusion.6 = f32[256,2048]{1,0:T(8,128)} fusion(bf16[256,2000]{0,1:T(8,128)(2,1)S(1)} %subtract_convert_fusion, bf16[2000,2048]{1,0:T(8,128)(2,1)} %param.6), kind=kOutput, calls=%fused_computation.30 | convolution fusion | flops 2097152000 | bytes 11313152 | tf_op jit(solution)/shard_map/dot_general | solution.py:26
  104.5 0.0 copy-done.1
  104.5 0.0 copy-start.2
  104.5 0.0 reduce-scatter.2.cloned.1.call-update
  104.5 0.0 all-gather.5.cloned.1.call-start
  104.5 0.7 all-gather.5.cloned.1.call-update
  105.2 0.0 copy-done.2
  105.3 0.2 convert_reduce_fusion
  105.4 0.1 select_reduce_fusion.1
  105.6 0.1 sub.44
  105.6 0.7 reshape.51
  106.3 3.2 %all-to-all-start = ((s32[4,1,128]{2,1,0:T(1,128)}), s32[4,1,128]{2,1,0:T(1,128)S(1)}, u32[]{:S(2)}, u32[]{:S(2)}) async-start(s32[4,1,128]{2,1,0:T(1,128)} %reshape.51), calls=%async_computation.1 | async-start | bytes 4096 | tf_op jit(solution)/shard_map/all_to_all | solution.py:63
  109.5 0.0 copy-done
  109.6 0.4 convolution_convert_fusion
  110.0 0.1 slice_bitcast_fusion.3
  110.0 0.9 pad_maximum_fusion
  110.9 2.3 %all-to-all-done = s32[4,1,128]{2,1,0:T(1,128)S(1)} async-done(((s32[4,1,128]{2,1,0:T(1,128)}), s32[4,1,128]{2,1,0:T(1,128)S(1)}, u32[]{:S(2)}, u32[]{:S(2)}) %all-to-all-start) | async-done | bytes 2080 | tf_op jit(solution)/shard_map/all_to_all | solution.py:63
  113.2 3.5 %all-to-all-start.2 = ((bf16[4,8,16,512]{3,2,1,0:T(8,128)(2,1)}), bf16[4,8,16,512]{3,2,1,0:T(8,128)(2,1)S(1)}, u32[]{:S(2)}, u32[]{:S(2)}) async-start(bf16[4,8,16,512]{3,2,1,0:T(8,128)(2,1)} %pad_maximum_fusion), calls=%async_computation.3 | async-start | bytes 1048576 | tf_op jit(solution)/shard_map/all_to_all | solution.py:52
  116.7 0.5 broadcast.29
  117.2 0.7 reduce.4
  117.9 0.1 reshape.52
  118.0 0.7 all_to_all.39
  118.6 6.8 %all-to-all-done.2 = bf16[4,8,16,512]{3,2,1,0:T(8,128)(2,1)S(1)} async-done(((bf16[4,8,16,512]{3,2,1,0:T(8,128)(2,1)}), bf16[4,8,16,512]{3,2,1,0:T(8,128)(2,1)S(1)}, u32[]{:S(2)}, u32[]{:S(2)}) %all-to-all-start.2) | async-done | bytes 524320 | tf_op jit(solution)/shard_map/all_to_all | solution.py:52
  125.5 3.3 %all-to-all-start.1 = ((s32[8,64,1]{1,2,0:T(1,128)}), s32[8,64,1]{1,2,0:T(1,128)S(1)}, u32[]{:S(2)}, u32[]{:S(2)}) async-start(s32[8,64,1]{1,2,0:T(1,128)} %bitcast.2), calls=%async_computation.2 | async-start | bytes 8192 | tf_op jit(solution)/shard_map/all_to_all | solution.py:62
  128.8 6.4 %all-to-all-done.1 = s32[8,64,1]{1,2,0:T(1,128)S(1)} async-done(((s32[8,64,1]{1,2,0:T(1,128)}), s32[8,64,1]{1,2,0:T(1,128)S(1)}, u32[]{:S(2)}, u32[]{:S(2)}) %all-to-all-start.1) | async-done | bytes 2080 | tf_op jit(solution)/shard_map/all_to_all | solution.py:62
  135.2 15.7 %all_to_all.52 = bf16[8,64,512]{2,1,0:T(8,128)(2,1)S(1)} all-to-all(bf16[8,64,512]{2,1,0:T(8,128)(2,1)S(1)} %bitcast.37), channel_id=1, replica_groups=mesh['dp'=4,'vocab'=8] {'vocab'}, dimensions={0} | all-to-all | bytes 1048576 | tf_op jit(solution)/shard_map/all_to_all | solution.py:50
  150.9 3.5 %all-to-all-start.4 = ((bf16[256,4,512]{0,2,1:T(8,128)(2,1)}), bf16[256,4,512]{0,2,1:T(8,128)(2,1)S(1)}, u32[]{:S(2)}, u32[]{:S(2)}) async-start(bf16[256,4,512]{0,2,1:T(8,128)(2,1)} %bitcast.11), calls=%async_computation.5 | async-start | bytes 2097152 | tf_op jit(solution)/shard_map/all_to_all | solution.py:78
  154.4 0.5 broadcast.27
  154.9 0.7 reduce.3
  155.6 0.1 eq.46
  155.7 3.1 %fusion = f32[2000,512]{1,0:T(8,128)} fusion(bf16[512,512]{1,0:T(8,128)(2,1)S(1)} %bitcast.40, s32[512]{0:T(512)S(1)} %eq.46), kind=kOutput, calls=%fused_computation.2 | convolution fusion | flops 1049600000 | bytes 4622336 | tf_op jit(solution)/shard_map/dot_general | solution.py:77
  158.8 0.6 add_subtract_fusion
  159.4 9.4 %all-to-all-done.4 = bf16[256,4,512]{0,2,1:T(8,128)(2,1)S(1)} async-done(((bf16[256,4,512]{0,2,1:T(8,128)(2,1)}), bf16[256,4,512]{0,2,1:T(8,128)(2,1)S(1)}, u32[]{:S(2)}, u32[]{:S(2)}) %all-to-all-start.4) | async-done | bytes 1048608 | tf_op jit(solution)/shard_map/all_to_all | solution.py:78
  168.8 0.5 copy.25
  169.4 4.4 %reduce-scatter.2.cloned.1.call-done = f32[256,256]{1,0:T(8,128)} async-done(((f32[256,2048]{1,0:T(8,128)}), f32[256,256]{1,0:T(8,128)}) %reduce-scatter.2.cloned.1.call-update) | async-done | bytes 262160 | tf_op jit(solution)/shard_map/reduce_scatter | solution.py:27
  173.8 1.6 convert_element_type.18
  175.4 34.0 %all-gather.5.cloned.1.call-done = bf16[1024,2000]{0,1:T(8,128)(2,1)} async-done(((bf16[256,2000]{0,1:T(8,128)(2,1)}), bf16[1024,2000]{0,1:T(8,128)(2,1)}) %all-gather.5.cloned.1.call-update) | async-done | bytes 4096016 | tf_op jit(solution)/shard_map/all_gather | solution.py:80
  209.4 7.0 %add_convert_fusion = bf16[2000,512]{1,0:T(8,128)(2,1)} fusion(f32[2000,512]{1,0:T(8,128)} %fusion, bf16[1024,2000]{0,1:T(8,128)(2,1)} %all-gather.5.cloned.1.call-done, bf16[1024,512]{1,0:T(8,128)(2,1)S(1)} %bitcast.39), kind=kOutput, calls=%fused_computation | convolution fusion | flops 2099200000 | bytes 11288576 | tf_op jit(solution)/shard_map/dot_general | solution.py:79
  (7 shorter events, 0.1 us)
Async XLA Ops:
  7.2 102.4 %copy-start = (bf16[64,2048]{1,0:T(8,128)(2,1)S(1)}, bf16[64,2048]{1,0:T(8,128)(2,1)}, u32[]{:S(2)}) copy-start(bf16[64,2048]{1,0:T(8,128)(2,1)} %param.9) | copy-start | bytes 786436
  7.2 46.5 %all-gather.3.cloned.1.call-start = ((), (), s32[]{:S(2)}) async-start(), calls=%async_computation.6 | async-start | bytes 1179648 | tf_op jit(solution)/shard_map/all_gather | solution.py:13
  8.9 164.8 %reduce-scatter.2.cloned.1.call-start = ((), (), s32[]{:S(2)}) async-start(), calls=%async_computation.7 | async-start | bytes 2359296 | tf_op jit(solution)/shard_map/reduce_scatter | solution.py:27
  97.0 7.5 %copy-start.1 = (bf16[256,2000]{0,1:T(8,128)(2,1)}, bf16[256,2000]{0,1:T(8,128)(2,1)S(1)}, u32[]{:S(2)}) copy-start(bf16[256,2000]{0,1:T(8,128)(2,1)S(1)} %subtract_convert_fusion) | copy-start | bytes 3072004
  104.5 0.8 copy-start.2
  104.5 104.9 %all-gather.5.cloned.1.call-start = ((), (), s32[]{:S(2)}) async-start(), calls=%async_computation.8 | async-start | bytes 5120000 | tf_op jit(solution)/shard_map/all_gather | solution.py:80
  106.3 6.9 %all-to-all-start = ((s32[4,1,128]{2,1,0:T(1,128)}), s32[4,1,128]{2,1,0:T(1,128)S(1)}, u32[]{:S(2)}, u32[]{:S(2)}) async-start(s32[4,1,128]{2,1,0:T(1,128)} %reshape.51), calls=%async_computation.1 | async-start | bytes 4096 | tf_op jit(solution)/shard_map/all_to_all | solution.py:63
  113.2 12.3 %all-to-all-start.2 = ((bf16[4,8,16,512]{3,2,1,0:T(8,128)(2,1)}), bf16[4,8,16,512]{3,2,1,0:T(8,128)(2,1)S(1)}, u32[]{:S(2)}, u32[]{:S(2)}) async-start(bf16[4,8,16,512]{3,2,1,0:T(8,128)(2,1)} %pad_maximum_fusion), calls=%async_computation.3 | async-start | bytes 1048576 | tf_op jit(solution)/shard_map/all_to_all | solution.py:52
  125.5 9.7 %all-to-all-start.1 = ((s32[8,64,1]{1,2,0:T(1,128)}), s32[8,64,1]{1,2,0:T(1,128)S(1)}, u32[]{:S(2)}, u32[]{:S(2)}) async-start(s32[8,64,1]{1,2,0:T(1,128)} %bitcast.2), calls=%async_computation.2 | async-start | bytes 8192 | tf_op jit(solution)/shard_map/all_to_all | solution.py:62
  150.9 17.9 %all-to-all-start.4 = ((bf16[256,4,512]{0,2,1:T(8,128)(2,1)}), bf16[256,4,512]{0,2,1:T(8,128)(2,1)S(1)}, u32[]{:S(2)}, u32[]{:S(2)}) async-start(bf16[256,4,512]{0,2,1:T(8,128)(2,1)} %bitcast.11), calls=%async_computation.5 | async-start | bytes 2097152 | tf_op jit(solution)/shard_map/all_to_all | solution.py:78
Sparse Core Ops, SparseCore 0:
  10.7 42.9 all-gather.2
  104.6 69.1 reduce-scatter.1
  175.9 33.4 all-gather.4
